TPU v7x, 32 devices: a whole 2x2x4 slice. The times are simulated.
32 devices in a mesh: rep: 2 (over x), tp: 8 (over z, y), sub: 2 (over core).
Axes of the slice: x: 2, y: 2, z: 4, core: 2. Of those that a mesh axis runs over, the one named last changes fastest.
Arguments:
- attention: bfloat16 [1024, 8192], P('rep', ('tp', 'sub')), parts along dimension 0, may hold values from -6 to 6
- out_weight: bfloat16 [8192, 8192], P(('tp', 'sub')), may hold values from -0.09375 to 0.09375
- residual: bfloat16 [1024, 8192], P('rep', ('tp', 'sub')), parts along dimension 0, may hold values from -6 to 6
- norm_gain: bfloat16 [8192], P(('tp', 'sub')), may hold values from 0.25 to 1.75
Outputs:
- quantized: bfloat16 [1024, 8192], P('rep'), parts along dimension 0
- scales: bfloat16 [1024, 64], P('rep'), parts along dimension 0
- new_residual: bfloat16 [1024, 8192], P('rep', ('tp', 'sub')), parts along dimension 0
There are 2 independent parts, one for each index of `rep`. A program takes and returns all parts, laid end to end along the dimension named above; an argument that names none is the same for every part. Nothing has to cross between parts.
All inputs are finite; a program needn't handle non-finite values.
Results may differ from a plain program's by a relative error of at most 0.0048.
Values may be sent and summed in bfloat16 or wider, within the bound.
A program may use at most 128 MiB of HBM per device.

v0:
```python
import jax
import jax.numpy as jnp
from jax import lax
from jax.sharding import PartitionSpec as P

BLOCK = 128


epsilon = 0.1
floor_scale = 0.5


def per_device(attention, out_weight, residual, norm_gain):
    width_all = out_weight.shape[1]
    summed = lax.psum_scatter(
        lax.dot_general(
            out_weight, attention, (((0,), (1,)), ((), ())), preferred_element_type=jnp.float32
        ),
        ("tp", "sub"),
        scatter_dimension=0,
        tiled=True,
    )
    hidden = residual.astype(jnp.float32) + summed.T
    new_residual = hidden.astype(jnp.bfloat16)
    squares = lax.psum(jnp.sum(hidden * hidden, axis=1), ("tp", "sub"))
    mean_square = squares / width_all
    normed = hidden * lax.rsqrt(mean_square + epsilon)[:, None] * norm_gain.astype(jnp.float32)
    blocks = normed.reshape(hidden.shape[0], hidden.shape[1] // BLOCK, BLOCK)
    largest = jnp.max(jnp.abs(blocks), axis=2)
    scales = jnp.maximum(largest, floor_scale).astype(jnp.bfloat16)
    quantized = (
        (blocks / scales.astype(jnp.float32)[:, :, None]).reshape(hidden.shape).astype(jnp.bfloat16)
    )
    full_quant, full_scales = (
        lax.all_gather(quantized, ("tp", "sub"), axis=1, tiled=True),
        lax.all_gather(scales, ("tp", "sub"), axis=1, tiled=True),
    )
    return (full_quant, full_scales, new_residual)


def solution(mesh):
    in_specs = (
        P("rep", ("tp", "sub")),
        P(("tp", "sub"), None),
        P("rep", ("tp", "sub")),
        P(("tp", "sub")),
    )
    out_specs = (P("rep", None), P("rep", None), P("rep", ("tp", "sub")))
    return jax.shard_map(
        per_device, mesh=mesh, in_specs=in_specs, out_specs=out_specs, check_vma=False
    )
```

profile of v0, /device:TPU:1, one launch (start us, length us, event | category | flops | bytes accessed | tf_op | source)
XLA Modules:
  0.0 327.1 jit_solution(3654953643072817745)
XLA Ops:
  7.2 0.0 copy-start
  7.2 0.0 reduce-scatter.2.cloned.1.call-start
  7.2 1.0 copy-done
  8.2 11.7 %fusion.5 = f32[8192,512]{1,0:T(8,128)} fusion(bf16[512,8192]{1,0:T(8,128)(2,1)} %param.5, bf16[512,512]{1,0:T(8,128)(2,1)S(1)} %copy-done), kind=kOutput, calls=%fused_computation.12 | convolution fusion | flops 4294967296 | bytes 25690112 | tf_op jit(solution)/shard_map/dot_general | solution.py:16
  19.9 0.0 copy-start.1
  19.9 0.0 copy-start.2
  19.9 0.0 reduce-scatter.2.cloned.1.call-update
  19.9 0.0 all-gather.3.cloned.1.call-start
  20.0 1.0 copy-done.1
  20.9 0.2 copy.10
  21.2 0.0 copy-done.2
  21.2 178.0 %reduce-scatter.2.cloned.1.call-done = f32[512,512]{1,0:T(8,128)} async-done(((f32[8192,512]{1,0:T(8,128)}), f32[512,512]{1,0:T(8,128)}) %reduce-scatter.2.cloned.1.call-update) | async-done | bytes 1048592 | tf_op jit(solution)/shard_map/reduce_scatter | solution.py:15
  199.2 1.4 multiply_reduce_fusion
  200.6 29.8 %psum.7 = f32[512]{0:T(512)S(1)} all-reduce(f32[512]{0:T(512)S(1)} %multiply_reduce_fusion), channel_id=1, replica_groups=mesh['rep'=2,'tp'=8,'sub'=2] {'tp','sub'}, use_global_device_ids=true, to_apply=%region_2.0 | all-reduce | flops 512 | bytes 4096 | tf_op jit(solution)/shard_map/psum | solution.py:25
  230.4 1.4 bitcast_reduce_fusion
  231.8 2.2 fusion.2
  234.1 0.0 all-gather.3.cloned.1.call-update
  234.1 1.0 copy.12
  235.1 20.3 %all-gather = bf16[16,4,512]{2,1,0:T(4,128)(2,1)S(1)} all-gather(bf16[1,4,512]{2,1,0:T(4,128)(2,1)S(1)} %get-tuple-element.11), channel_id=1, replica_groups=mesh['rep'=2,'tp'=8,'sub'=2] {'tp','sub'}, dimensions={0}, use_global_device_ids=true | all-gather | bytes 69632 | tf_op jit(solution)/shard_map/all_gather | solution.py:36
  255.4 0.6 reshape.18
  256.1 52.2 %all-gather.3.cloned.1.call-done = bf16[512,8192]{0,1:T(8,128)(2,1)} async-done(((bf16[512,512]{0,1:T(8,128)(2,1)}), bf16[512,8192]{0,1:T(8,128)(2,1)}) %all-gather.3.cloned.1.call-update) | async-done | bytes 8388624 | tf_op jit(solution)/shard_map/all_gather | solution.py:35
  308.3 11.9 %copy.11 = bf16[512,8192]{1,0:T(8,128)(2,1)} copy(bf16[512,8192]{0,1:T(8,128)(2,1)} %all-gather.3.cloned.1.call-done) | data formatting | bytes 16777216
  (3 shorter events, 0.0 us)
Async XLA Ops:
  7.2 1.0 copy-start
  7.2 192.0 %reduce-scatter.2.cloned.1.call-start = ((), (), s32[]{:S(2)}) async-start(), calls=%async_computation.1 | async-start | bytes 17825792 | tf_op jit(solution)/shard_map/reduce_scatter | solution.py:15
  19.9 1.0 copy-start.1
  19.9 1.3 copy-start.2
  19.9 288.4 %all-gather.3.cloned.1.call-start = ((), (), s32[]{:S(2)}) async-start(), calls=%async_computation.2 | async-start | bytes 8912896 | tf_op jit(solution)/shard_map/all_gather | solution.py:35
Sparse Core Ops, SparseCore 0:
  20.0 179.0 reduce-scatter.1
  234.2 74.0 all-gather.2
where the time goes:
time: 328 us; the launch traced here: 327 us
  waiting for transfers between devices  230 us (70%)
  blocking collectives  50.1 us (15%)
  local copies, waits for them, and re-layouts  15.7 us (5%)
  between operations  14.1 us (4%)
  matrix products  11.7 us (4%)
  other arithmetic  5.1 us (2%)
    reduce_scatter x1, waiting for transfers between devices, per_device(): lax.psum_scatter(lax.dot_general(out_weight, attention, (((0,), (1,)), ((...  178 us
    all_gather x1, waiting for transfers between devices, per_device(): lax.all_gather(quantized, ('tp', 'sub'), axis=1, tiled=True)  52.2 us
    psum x1, blocking collectives, per_device(): squares = lax.psum(jnp.sum(hidden * hidden, axis=1), ('tp', 'sub'))  29.8 us
    all_gather x1, blocking collectives, per_device(): lax.all_gather(scales, ('tp', 'sub'), axis=1, tiled=True)  20.3 us
    unnamed x10, local copies, waits for them, and re-layouts  15.7 us
    dot_general x1, matrix products, per_device(): lax.dot_general(out_weight, attention, (((0,), (1,)), ((), ())), preferre...  11.7 us
  transfers between devices with their start and end apart: 2, of which 2 were waited for; matrix products, arithmetic and copies ran while one was open for 1% of the time, Pallas kernels for 0%

commit v1 on v0

v1 whole, which is shorter than its diff:
```python
import functools

import jax
import jax.numpy as jnp
from jax import lax
from jax.experimental import pallas as pl
from jax.experimental.pallas import tpu as pltpu
from jax.sharding import PartitionSpec as P

BLOCK = 128
LANES = 128
MESH = pl.DeviceIdType.MESH

epsilon = 0.1
floor_scale = 0.5


def loop(n, body):
    if n <= 8:
        for i in range(n):
            body(i)
    else:
        lax.fori_loop(0, n, lambda i, c: (body(i), c)[1], 0)


def kernel(
    Y, Z, U, C, R, width_all,
    att, weight, res, gain,
    quant, scales, new_res,
    att_p, w_own, w_par, ysend, ybuf, zsend, zbuf, hid, stat, sct, scfull,
    l_sem, xs_sem, xr_sem, as_sem, ar_sem, ys_sem, yr_sem, zs_sem, zr_sem,
    ss_sem, sr_sem, cs_sem, cr_sem, qzs, qzr, qys, qyr, qus, qur,
):
    T = Y * Z
    n = T * U
    w = res.shape[1]
    nb = w // BLOCK
    tp = lax.axis_index("tp")
    s = lax.axis_index("sub")
    z = tp // Y
    y = lax.rem(tp, Y)
    me = tp * U + s
    other = (U - 1) - s
    f32 = jnp.float32

    def cols(t, sub):
        return pl.ds(pl.multiple_of((t * U + sub) * w, w), w)

    def rows(c):
        return pl.ds(c * R, R)

    def rc(src, dst, ss, rs, t, sub):
        return pltpu.make_async_remote_copy(
            src_ref=src, dst_ref=dst, send_sem=ss, recv_sem=rs,
            device_id={"tp": t, "sub": sub}, device_id_type=MESH,
        )

    yp = (Y - 1) - y
    zt = lambda zz: zz * Y + y
    zo = lambda k: lax.rem(z + k, Z)
    order = lambda i: (i % Z) * Y + (yp if i < Z else y) if Y > 1 else i

    def wload(t):
        return pltpu.make_async_copy(weight.at[:, cols(t, s)], w_own.at[t], l_sem.at[t])

    def wpush(t):
        return rc(weight.at[:, cols(t, other)], w_par.at[t], xs_sem.at[t], xr_sem.at[t], tp, other)

    apush = rc(att, att_p, as_sem, ar_sem, tp, other)

    loop(T, lambda i: wload(order(i)).start())
    barrier = pltpu.get_barrier_semaphore()

    def greet(k):
        p = lax.rem(me + k + 1, n)
        pl.semaphore_signal(
            barrier, inc=1, device_id={"tp": p // U, "sub": lax.rem(p, U)}, device_id_type=MESH
        )

    loop(n - 1, greet)
    pl.semaphore_wait(barrier, n - 1)
    apush.start()
    loop(T, lambda i: wpush(order(i)).start())
    apush.wait()

    def w_wait(t):
        wload(t).wait()
        wpush(t).wait_recv()

    def product(c, t):
        a = jnp.dot(att[rows(c), :], w_own[t], preferred_element_type=f32)
        return a + jnp.dot(att_p[rows(c), :], w_par[t], preferred_element_type=f32)

    def ycopy(c):
        return rc(ysend.at[c], ybuf.at[c], ys_sem.at[c], yr_sem.at[c], z * Y + yp, s)

    def zcopy(c, zz):
        return rc(zsend.at[c, zz], zbuf.at[c, z], zs_sem.at[c, zz], zr_sem.at[c, z], zt(zz), s)

    def zwait(c, zz):
        rc(zsend.at[c, zz], zbuf.at[c, zz], zs_sem.at[c, zz], zr_sem.at[c, zz], zt(zz), s).wait_recv()

    if Y > 1:
        for c in range(C):
            def one(zz, c=c):
                t = zz * Y + yp
                if c == 0:
                    w_wait(t)
                ysend[c, zz] = product(c, t).astype(ysend.dtype)
            loop(Z, one)
            ycopy(c).start()

    def s4(c):
        if Y > 1:
            ycopy(c).wait_recv()

        def total(zz):
            t = zt(zz)
            if c == 0:
                w_wait(t)
            a = product(c, t)
            if Y > 1:
                a = a + ybuf[c, zz].astype(f32)
            return a

        def one(k):
            zz = zo(k + 1)
            zsend[c, zz] = total(zz).astype(zsend.dtype)
            zcopy(c, zz).start()

        loop(Z - 1, one)
        hid[c] = total(z) + res[rows(c), :].astype(f32)

    def peer(k):
        p = lax.rem(me + k + 1, n)
        return p, p // U, lax.rem(p, U)

    def scopy(c, p, t, u, slot):
        return rc(stat.at[c, me], stat.at[c, slot], ss_sem.at[c, p], sr_sem.at[c, slot], t, u)

    def ccopy(c, p, t, u, slot):
        return rc(sct.at[c, me], sct.at[c, slot], cs_sem.at[c, p], cr_sem.at[c, slot], t, u)

    def s5(c):
        def add(k):
            zz = zo(k + 1)
            zwait(c, zz)
            hid[c] = hid[c] + zbuf[c, zz].astype(f32)

        loop(Z - 1, add)
        h = hid[c]
        new_res[rows(c), :] = h.astype(new_res.dtype)
        sq = jnp.sum(h * h, axis=1, keepdims=True)
        stat[c, me] = jnp.broadcast_to(sq, (R, LANES)).T[0:1, :]

        def send(k):
            p, t, u = peer(k)
            scopy(c, p, t, u, me).start()

        loop(n - 1, send)

    def qz(c, zz):
        sl = quant.at[rows(c), cols(tp, s)]
        return rc(sl, sl, qzs.at[c, zz], qzr.at[c, z], zt(zz), s)

    def qz_wait(c, zz):
        sl = quant.at[rows(c), cols(zt(zz), s)]
        rc(sl, sl, qzs.at[c, zz], qzr.at[c, zz], zt(zz), s).wait_recv()

    def qy(c, zz, yy):
        sl = quant.at[rows(c), cols(zz * Y + yy, s)]
        return rc(sl, sl, qys.at[c, zz], qyr.at[c, zz], z * Y + yp, s)

    def qu(c, t, u):
        sl = quant.at[rows(c), cols(t, u)]
        return rc(sl, sl, qus.at[c, t], qur.at[c, t], tp, other)

    def s6(c):
        def w_stat(k):
            p, t, u = peer(k)
            scopy(c, p, t, u, p).wait_recv()

        loop(n - 1, w_stat)
        tot = jnp.sum(stat[c], axis=0)
        col = jnp.broadcast_to(tot, (LANES, R)).T
        inv = lax.rsqrt(col / width_all + epsilon)
        for j in range(nb):
            sl = slice(j * BLOCK, (j + 1) * BLOCK)
            nr = hid[c, :, sl] * inv * gain[:, sl].astype(f32)
            sc = jnp.maximum(jnp.max(jnp.abs(nr), axis=1, keepdims=True), floor_scale)
            sc = jnp.broadcast_to(sc.astype(jnp.bfloat16).astype(f32), (R, BLOCK))
            quant[rows(c), pl.ds(pl.multiple_of(me * w + j * BLOCK, BLOCK), BLOCK)] = (
                nr / sc
            ).astype(quant.dtype)
            sct[c, me, j : j + 1, :] = sc.T[0:1, :]
        loop(Z - 1, lambda k: qz(c, zo(k + 1)).start())
        if Y > 1:
            qy(c, z, y).start()

        def send(k):
            p, t, u = peer(k)
            ccopy(c, p, t, u, me).start()

        loop(n - 1, send)
        qu(c, tp, s).start()

    def s7(c):
        def one(k):
            zz = zo(k + 1)
            qz_wait(c, zz)
            if Y > 1:
                qy(c, zz, y).start()
            qu(c, zt(zz), s).start()

        loop(Z - 1, one)

    def s8(c):
        if Y > 1:
            def one(k):
                zz = zo(k)
                qy(c, zz, yp).wait_recv()
                qu(c, zz * Y + yp, s).start()

            loop(Z, one)

    def s9(c):
        def w_c(k):
            p, t, u = peer(k)
            ccopy(c, p, t, u, p).wait_recv()

        loop(n - 1, w_c)
        for d in range(n):
            scfull[d * nb : (d + 1) * nb, :] = sct[c, d]
        scales[rows(c), :] = scfull[...].T[:, : n * nb].astype(scales.dtype)
        loop(T, lambda t: qu(c, t, other).wait_recv())

    stages = (s4, s5, s6, s7, s8, s9)
    for i in range(C + len(stages) - 1):
        for j, stage in enumerate(stages):
            if 0 <= i - j < C:
                stage(i - j)

    loop(T, lambda t: wpush(t).wait_send())
    for c in range(C):
        if Y > 1:
            ycopy(c).wait_send()
            loop(Z, lambda zz, c=c: qy(c, zz, y).wait_send())

        def zdone(k, c=c):
            zcopy(c, zo(k + 1)).wait_send()
            qz(c, zo(k + 1)).wait_send()

        loop(Z - 1, zdone)

        def pdone(k, c=c):
            p, t, u = peer(k)
            scopy(c, p, t, u, me).wait_send()
            ccopy(c, p, t, u, me).wait_send()

        loop(n - 1, pdone)
        loop(T, lambda t, c=c: qu(c, t, s).wait_send())


def per_device(Y, Z, U, attention, out_weight, residual, norm_gain):
    M, K = attention.shape
    width_all = out_weight.shape[1]
    w = residual.shape[1]
    T = Y * Z
    n = T * U
    R = LANES
    C = M // R
    nb = w // BLOCK
    bf = jnp.bfloat16
    dma = pltpu.SemaphoreType.DMA
    vm = pl.BlockSpec(memory_space=pltpu.VMEM)
    return pl.pallas_call(
        functools.partial(kernel, Y, Z, U, C, R, width_all),
        out_shape=(
            jax.ShapeDtypeStruct((M, width_all), bf),
            jax.ShapeDtypeStruct((M, width_all // BLOCK), bf),
            jax.ShapeDtypeStruct((M, w), bf),
        ),
        in_specs=[vm, pl.BlockSpec(memory_space=pl.ANY), vm, vm],
        out_specs=(vm, vm, vm),
        scratch_shapes=[
            pltpu.VMEM((M, K), bf),
            pltpu.VMEM((T, K, w), bf),
            pltpu.VMEM((T, K, w), bf),
            pltpu.VMEM((C, Z, R, w), bf),
            pltpu.VMEM((C, Z, R, w), bf),
            pltpu.VMEM((C, Z, R, w), bf),
            pltpu.VMEM((C, Z, R, w), bf),
            pltpu.VMEM((C, R, w), jnp.float32),
            pltpu.VMEM((C, n, 1, R), jnp.float32),
            pltpu.VMEM((C, n, nb, R), jnp.float32),
            pltpu.VMEM((-(-n * nb // LANES) * LANES, R), jnp.float32),
            dma((T,)), dma((T,)), dma((T,)), dma, dma,
            dma((C,)), dma((C,)), dma((C, Z)), dma((C, Z)),
            dma((C, n)), dma((C, n)), dma((C, n)), dma((C, n)),
            dma((C, Z)), dma((C, Z)), dma((C, Z)), dma((C, Z)), dma((C, T)), dma((C, T)),
        ],
        compiler_params=pltpu.CompilerParams(
            collective_id=0, has_side_effects=True, vmem_limit_bytes=60 * 1024 * 1024
        ),
        cost_estimate=pl.CostEstimate(
            flops=2 * M * K * width_all, bytes_accessed=2 * K * width_all, transcendentals=0
        ),
    )(attention, out_weight, residual, norm_gain.reshape(1, w))


def inner_count(mesh):
    chips = [tuple(getattr(d, "coords", (0, 0, i))) for i, d in enumerate(mesh.devices[0, :, 0].flat)]
    count = sum(1 for c in chips if c[2] == chips[0][2])
    return count if len(chips) % count == 0 and count <= 2 else 1


def solution(mesh):
    Y = inner_count(mesh)
    Z = mesh.shape["tp"] // Y
    in_specs = (
        P("rep", ("tp", "sub")),
        P(("tp", "sub"), None),
        P("rep", ("tp", "sub")),
        P(("tp", "sub")),
    )
    out_specs = (P("rep", None), P("rep", None), P("rep", ("tp", "sub")))
    return jax.shard_map(
        functools.partial(per_device, Y, Z, mesh.shape["sub"]),
        mesh=mesh, in_specs=in_specs, out_specs=out_specs, check_vma=False,
    )
```

time: 328 us -> 153 us (0.47)
  the two profiles are of different devices: /device:TPU:1 before, /device:TPU:9 now
where the time goes in v1:
time: 153 us
  Pallas kernels  141 us (92%)
  local copies, waits for them, and re-layouts  11.5 us (8%)
    pallas_call x1, Pallas kernels, per_device(): pl.pallas_call(functools.partial(kernel, Y, Z, U, C, R, width_all), out_s...  141 us
    unnamed x4, local copies, waits for them, and re-layouts  8.63 us

profile of v1, /device:TPU:9, one launch (start us, length us, event | category | flops | bytes accessed | tf_op | source)
XLA Modules:
  0.0 152.7 jit_solution(6997655707747898507)
XLA Ops:
  0.6 1.3 reshape.9.gain
  1.9 140.5 %shard_map.67 = (bf16[512,8192]{1,0:T(8,128)(2,1)}, bf16[512,64]{1,0:T(8,128)(2,1)}, bf16[512,512]{1,0:T(8,128)(2,1)}) custom-call(bf16[512,512]{1,0:T(8,128)(2,1)} %att.1, bf16[512,8192]{1,0:T(8,128)(2,1)} %weight.1, bf16[512,512]{1,0:T(8,128)(2,1)} %res.1, bf16[1,512]{1,0:T(2,128)(2,1)} %reshape.9.gain), custom_call_target="tpu_custom_call" | custom-call | flops 4294967296 | bytes 8388608 | tf_op jit(solution)/shard_map/pallas_call | solution.py:276
  142.4 1.6 %copy.7 = bf16[512,64]{0,1:T(8,128)(2,1)} copy(bf16[512,64]{1,0:T(8,128)(2,1)} %get-tuple-element.4) | data formatting | bytes 131072 | tf_op jit(solution)/shard_map/pallas_call | solution.py:276
  144.0 0.0 copy-start
  144.0 7.8 %copy.10 = bf16[512,8192]{1,0:T(8,128)(2,1)} copy(bf16[512,8192]{1,0:T(8,128)(2,1)} %get-tuple-element.9) | data formatting | bytes 16777216
  151.9 0.0 copy-done
  151.9 0.8 copy.11
Async XLA Ops:
  144.0 7.8 %copy-start = (bf16[512,512]{1,0:T(8,128)(2,1)S(1)}, bf16[512,512]{1,0:T(8,128)(2,1)}, u32[]{:S(2)}) copy-start(bf16[512,512]{1,0:T(8,128)(2,1)} %get-tuple-element.11) | copy-start | bytes 1572868

commit v2 on v1

--- a/solution.py
+++ b/solution.py
@@ -9,6 +9,8 @@
 
 BLOCK = 128
 LANES = 128
+ROWS_STEP = 128
+GRANT = 40 * 1024 * 1024
 MESH = pl.DeviceIdType.MESH
 
 epsilon = 0.1
@@ -26,10 +28,10 @@
 def kernel(
     Y, Z, U, C, R, width_all,
     att, weight, res, gain,
-    quant, scales, new_res,
-    att_p, w_own, w_par, ysend, ybuf, zsend, zbuf, hid, stat, sct, scfull,
+    quant, stat, new_res,
+    att_p, w_own, w_par, ysend, ybuf, zsend, zbuf, hid,
     l_sem, xs_sem, xr_sem, as_sem, ar_sem, ys_sem, yr_sem, zs_sem, zr_sem,
-    ss_sem, sr_sem, cs_sem, cr_sem, qzs, qzr, qys, qyr, qus, qur,
+    ss_sem, sr_sem, qzs, qzr, qys, qyr, qus, qur,
 ):
     T = Y * Z
     n = T * U
@@ -49,6 +51,11 @@
     def rows(c):
         return pl.ds(c * R, R)
 
+    F = LANES // R
+
+    def sub_rows(c):
+        return pl.ds((c % F) * R, R)
+
     def rc(src, dst, ss, rs, t, sub):
         return pltpu.make_async_remote_copy(
             src_ref=src, dst_ref=dst, send_sem=ss, recv_sem=rs,
@@ -129,43 +136,20 @@
             zcopy(c, zz).start()
 
         loop(Z - 1, one)
-        hid[c] = total(z) + res[rows(c), :].astype(f32)
+        hid[c // F, sub_rows(c), :] = total(z) + res[rows(c), :].astype(f32)
 
     def peer(k):
         p = lax.rem(me + k + 1, n)
         return p, p // U, lax.rem(p, U)
 
-    def scopy(c, p, t, u, slot):
-        return rc(stat.at[c, me], stat.at[c, slot], ss_sem.at[c, p], sr_sem.at[c, slot], t, u)
-
-    def ccopy(c, p, t, u, slot):
-        return rc(sct.at[c, me], sct.at[c, slot], cs_sem.at[c, p], cr_sem.at[c, slot], t, u)
-
-    def s5(c):
-        def add(k):
-            zz = zo(k + 1)
-            zwait(c, zz)
-            hid[c] = hid[c] + zbuf[c, zz].astype(f32)
-
-        loop(Z - 1, add)
-        h = hid[c]
-        new_res[rows(c), :] = h.astype(new_res.dtype)
-        sq = jnp.sum(h * h, axis=1, keepdims=True)
-        stat[c, me] = jnp.broadcast_to(sq, (R, LANES)).T[0:1, :]
-
-        def send(k):
-            p, t, u = peer(k)
-            scopy(c, p, t, u, me).start()
-
-        loop(n - 1, send)
-
-    def qz(c, zz):
-        sl = quant.at[rows(c), cols(tp, s)]
-        return rc(sl, sl, qzs.at[c, zz], qzr.at[c, z], zt(zz), s)
-
-    def qz_wait(c, zz):
+    def scopy(g, p, t, u, slot):
+        return rc(stat.at[g, me], stat.at[g, slot], ss_sem.at[g, p], sr_sem.at[g, slot], t, u)
+
+    def qz(c, zz, right):
         sl = quant.at[rows(c), cols(zt(zz), s)]
-        rc(sl, sl, qzs.at[c, zz], qzr.at[c, zz], zt(zz), s).wait_recv()
+        to = jnp.minimum(z + 1, Z - 1) if right else jnp.maximum(z - 1, 0)
+        d = 1 if right else 0
+        return rc(sl, sl, qzs.at[c, zz, d], qzr.at[c, zz], zt(to), s)
 
     def qy(c, zz, yy):
         sl = quant.at[rows(c), cols(zz * Y + yy, s)]
@@ -175,42 +159,64 @@
         sl = quant.at[rows(c), cols(t, u)]
         return rc(sl, sl, qus.at[c, t], qur.at[c, t], tp, other)
 
-    def s6(c):
-        def w_stat(k):
-            p, t, u = peer(k)
-            scopy(c, p, t, u, p).wait_recv()
-
-        loop(n - 1, w_stat)
-        tot = jnp.sum(stat[c], axis=0)
-        col = jnp.broadcast_to(tot, (LANES, R)).T
-        inv = lax.rsqrt(col / width_all + epsilon)
-        for j in range(nb):
-            sl = slice(j * BLOCK, (j + 1) * BLOCK)
-            nr = hid[c, :, sl] * inv * gain[:, sl].astype(f32)
-            sc = jnp.maximum(jnp.max(jnp.abs(nr), axis=1, keepdims=True), floor_scale)
-            sc = jnp.broadcast_to(sc.astype(jnp.bfloat16).astype(f32), (R, BLOCK))
-            quant[rows(c), pl.ds(pl.multiple_of(me * w + j * BLOCK, BLOCK), BLOCK)] = (
-                nr / sc
-            ).astype(quant.dtype)
-            sct[c, me, j : j + 1, :] = sc.T[0:1, :]
-        loop(Z - 1, lambda k: qz(c, zo(k + 1)).start())
+    can_right, can_left = z < Z - 1, z > 0
+
+    def s5(c):
+        h = hid[c // F, sub_rows(c), :]
+        for k in range(Z - 1) if Z <= 8 else ():
+            zz = zo(k + 1)
+            zwait(c, zz)
+            h = h + zbuf[c, zz].astype(f32)
+        if Z > 8:
+            def add(k, h):
+                zz = zo(k + 1)
+                zwait(c, zz)
+                return h + zbuf[c, zz].astype(f32)
+
+            h = lax.fori_loop(0, Z - 1, add, h)
+        hid[c // F, sub_rows(c), :] = h
+        new_res[rows(c), :] = h.astype(new_res.dtype)
+        quant[rows(c), cols(tp, s)] = (h * gain[...].astype(f32)).astype(quant.dtype)
+        pl.when(can_right)(lambda: qz(c, z, True).start())
+        pl.when(can_left)(lambda: qz(c, z, False).start())
         if Y > 1:
             qy(c, z, y).start()
-
-        def send(k):
-            p, t, u = peer(k)
-            ccopy(c, p, t, u, me).start()
-
-        loop(n - 1, send)
         qu(c, tp, s).start()
+        if c % F == F - 1:
+            g = c // F
+            h = hid[g]
+            sq = jnp.sum(h * h, axis=1, keepdims=True)
+            stat[g, me, 0:1, :] = jnp.broadcast_to(sq, (LANES, LANES)).T[0:1, :]
+            for j in range(nb):
+                sl = slice(j * BLOCK, (j + 1) * BLOCK)
+                top = jnp.max(jnp.abs(h[:, sl] * gain[:, sl].astype(f32)), axis=1, keepdims=True)
+                stat[g, me, j + 1 : j + 2, :] = jnp.broadcast_to(top, (LANES, LANES)).T[0:1, :]
+
+            def send(k):
+                p, t, u = peer(k)
+                scopy(g, p, t, u, me).start()
+
+            loop(n - 1, send)
 
     def s7(c):
         def one(k):
-            zz = zo(k + 1)
-            qz_wait(c, zz)
-            if Y > 1:
-                qy(c, zz, y).start()
-            qu(c, zt(zz), s).start()
+            lo, hi = z - (k + 1), z + (k + 1)
+
+            @pl.when(lo >= 0)
+            def _():
+                qz(c, lo, True).wait_recv()
+                pl.when(can_right)(lambda: qz(c, lo, True).start())
+                if Y > 1:
+                    qy(c, lo, y).start()
+                qu(c, zt(lo), s).start()
+
+            @pl.when(hi < Z)
+            def _():
+                qz(c, hi, False).wait_recv()
+                pl.when(can_left)(lambda: qz(c, hi, False).start())
+                if Y > 1:
+                    qy(c, hi, y).start()
+                qu(c, zt(hi), s).start()
 
         loop(Z - 1, one)
 
@@ -224,17 +230,15 @@
             loop(Z, one)
 
     def s9(c):
-        def w_c(k):
-            p, t, u = peer(k)
-            ccopy(c, p, t, u, p).wait_recv()
-
-        loop(n - 1, w_c)
-        for d in range(n):
-            scfull[d * nb : (d + 1) * nb, :] = sct[c, d]
-        scales[rows(c), :] = scfull[...].T[:, : n * nb].astype(scales.dtype)
         loop(T, lambda t: qu(c, t, other).wait_recv())
-
-    stages = (s4, s5, s6, s7, s8, s9)
+        if c % F == F - 1:
+            def w_stat(k):
+                p, t, u = peer(k)
+                scopy(c // F, p, t, u, p).wait_recv()
+
+            loop(n - 1, w_stat)
+
+    stages = (s4, s5, s7, s8, s9)
     for i in range(C + len(stages) - 1):
         for j, stage in enumerate(stages):
             if 0 <= i - j < C:
@@ -245,20 +249,35 @@
         if Y > 1:
             ycopy(c).wait_send()
             loop(Z, lambda zz, c=c: qy(c, zz, y).wait_send())
-
-        def zdone(k, c=c):
-            zcopy(c, zo(k + 1)).wait_send()
-            qz(c, zo(k + 1)).wait_send()
-
-        loop(Z - 1, zdone)
-
-        def pdone(k, c=c):
-            p, t, u = peer(k)
-            scopy(c, p, t, u, me).wait_send()
-            ccopy(c, p, t, u, me).wait_send()
-
-        loop(n - 1, pdone)
+        loop(Z - 1, lambda k, c=c: zcopy(c, zo(k + 1)).wait_send())
+
+        def zdone(zz, c=c):
+            pl.when(can_right & (zz <= z))(lambda: qz(c, zz, True).wait_send())
+            pl.when(can_left & (zz >= z))(lambda: qz(c, zz, False).wait_send())
+
+        loop(Z, zdone)
         loop(T, lambda t, c=c: qu(c, t, s).wait_send())
+        if c % F == F - 1:
+            def pdone(k, c=c):
+                p, t, u = peer(k)
+                scopy(c // F, p, t, u, me).wait_send()
+
+            loop(n - 1, pdone)
+
+
+def finish(width_all, nb, hb, stat, res_in, quant, scales_t, res_out, full):
+    n = stat.shape[1]
+    total = jnp.sum(stat[0, :, 0:1, :], axis=0)
+    inv = lax.rsqrt(total / width_all + epsilon)
+    for d in range(n):
+        full[d * nb : (d + 1) * nb, :] = stat[0, d, 1:, :]
+    sc = jnp.maximum(full[...] * inv, floor_scale).astype(jnp.bfloat16)
+    scales_t[...] = sc[: n * nb, :]
+    factor = (inv / sc.astype(jnp.float32)).T
+    for j in range(n * nb):
+        sl = slice(j * BLOCK, (j + 1) * BLOCK)
+        quant[:, sl] = (hb[:, sl].astype(jnp.float32) * factor[:, j : j + 1]).astype(quant.dtype)
+    res_out[...] = res_in[...]
 
 
 def per_device(Y, Z, U, attention, out_weight, residual, norm_gain):
@@ -267,18 +286,20 @@
     w = residual.shape[1]
     T = Y * Z
     n = T * U
-    R = LANES
+    R = ROWS_STEP
     C = M // R
+    G = M // LANES
     nb = w // BLOCK
     bf = jnp.bfloat16
+    f32 = jnp.float32
     dma = pltpu.SemaphoreType.DMA
     vm = pl.BlockSpec(memory_space=pltpu.VMEM)
-    return pl.pallas_call(
+    hb, stat, kept = pl.pallas_call(
         functools.partial(kernel, Y, Z, U, C, R, width_all),
         out_shape=(
-            jax.ShapeDtypeStruct((M, width_all), bf),
-            jax.ShapeDtypeStruct((M, width_all // BLOCK), bf),
-            jax.ShapeDtypeStruct((M, w), bf),
+            pltpu.VMEM((M, width_all), bf),
+            pltpu.VMEM((G, n, 1 + nb, LANES), f32),
+            pltpu.VMEM((M, w), bf),
         ),
         in_specs=[vm, pl.BlockSpec(memory_space=pl.ANY), vm, vm],
         out_specs=(vm, vm, vm),
@@ -290,22 +311,41 @@
             pltpu.VMEM((C, Z, R, w), bf),
             pltpu.VMEM((C, Z, R, w), bf),
             pltpu.VMEM((C, Z, R, w), bf),
-            pltpu.VMEM((C, R, w), jnp.float32),
-            pltpu.VMEM((C, n, 1, R), jnp.float32),
-            pltpu.VMEM((C, n, nb, R), jnp.float32),
-            pltpu.VMEM((-(-n * nb // LANES) * LANES, R), jnp.float32),
+            pltpu.VMEM((G, LANES, w), f32),
             dma((T,)), dma((T,)), dma((T,)), dma, dma,
             dma((C,)), dma((C,)), dma((C, Z)), dma((C, Z)),
-            dma((C, n)), dma((C, n)), dma((C, n)), dma((C, n)),
-            dma((C, Z)), dma((C, Z)), dma((C, Z)), dma((C, Z)), dma((C, T)), dma((C, T)),
+            dma((G, n)), dma((G, n)),
+            dma((C, Z, 2)), dma((C, Z)), dma((C, Z)), dma((C, Z)), dma((C, T)), dma((C, T)),
         ],
         compiler_params=pltpu.CompilerParams(
-            collective_id=0, has_side_effects=True, vmem_limit_bytes=60 * 1024 * 1024
+            collective_id=0, has_side_effects=True, vmem_limit_bytes=GRANT
         ),
         cost_estimate=pl.CostEstimate(
             flops=2 * M * K * width_all, bytes_accessed=2 * K * width_all, transcendentals=0
         ),
     )(attention, out_weight, residual, norm_gain.reshape(1, w))
+    quant, scales_t, new_res = pl.pallas_call(
+        functools.partial(finish, width_all, nb),
+        grid=(G,),
+        out_shape=(
+            jax.ShapeDtypeStruct((M, width_all), bf),
+            jax.ShapeDtypeStruct((n * nb, M), bf),
+            jax.ShapeDtypeStruct((M, w), bf),
+        ),
+        in_specs=[
+            pl.BlockSpec((LANES, width_all), lambda i: (i, 0)),
+            pl.BlockSpec((1, n, 1 + nb, LANES), lambda i: (i, 0, 0, 0)),
+            pl.BlockSpec((LANES, w), lambda i: (i, 0)),
+        ],
+        out_specs=(
+            pl.BlockSpec((LANES, width_all), lambda i: (i, 0)),
+            pl.BlockSpec((n * nb, LANES), lambda i: (0, i)),
+            pl.BlockSpec((LANES, w), lambda i: (i, 0)),
+        ),
+        scratch_shapes=[pltpu.VMEM((-(-n * nb // LANES) * LANES, LANES), f32)],
+        compiler_params=pltpu.CompilerParams(vmem_limit_bytes=24 * 1024 * 1024),
+    )(hb, stat, kept)
+    return quant, scales_t.T, new_res
 
 
 def inner_count(mesh):

time: 153 us -> 132 us (0.86)
  the two profiles are of different devices: /device:TPU:9 before, /device:TPU:1 now
where the time goes in v2:
time: 132 us; the launch traced here: 131 us
  Pallas kernels  128 us (97%)
  local copies, waits for them, and re-layouts  2.77 us (2%)
    pallas_call x1, Pallas kernels, per_device(): pl.pallas_call(functools.partial(kernel, Y, Z, U, C, R, width_all), out_s...  121 us
    pallas_call x1, Pallas kernels, per_device(): pl.pallas_call(functools.partial(finish, width_all, nb), grid=(G,), out_s...  7.04 us

profile of v2, /device:TPU:1, one launch (start us, length us, event | category | flops | bytes accessed | tf_op | source)
XLA Modules:
  0.0 131.5 jit_solution(8927898286351113153)
XLA Ops:
  0.6 0.7 reshape.9.gain
  1.3 0.0 copy-start
  1.3 1.0 copy-done
  2.4 0.0 copy-start.1
  2.4 1.0 copy-done.1
  3.4 121.0 %shard_map.67 = (bf16[512,8192]{1,0:T(8,128)(2,1)S(1)}, f32[4,16,5,128]{3,2,1,0:T(8,128)S(1)}, bf16[512,512]{1,0:T(8,128)(2,1)S(1)}) custom-call(bf16[512,512]{1,0:T(8,128)(2,1)S(1)} %copy-done, bf16[512,8192]{1,0:T(8,128)(2,1)} %weight.1, bf16[512,512]{1,0:T(8,128)(2,1)S(1)} %copy-done.1, bf16[1,512]{1,0:T(2,128)(2,1)S(1)} %reshape.9.gain), custom_call_target="tpu_custom_call" | custom-call | flops 4294967296 | bytes 8388608 | tf_op jit(solution)/shard_map/pallas_call | solution.py:297
  124.4 7.0 %shard_map.68 = (bf16[512,8192]{1,0:T(8,128)(2,1)}, bf16[64,512]{1,0:T(8,128)(2,1)}, bf16[512,512]{1,0:T(8,128)(2,1)}) custom-call(bf16[512,8192]{1,0:T(8,128)(2,1)S(1)} %get-tuple-element.9.hb, f32[4,16,5,128]{3,2,1,0:T(8,128)S(1)} %get-tuple-element.10.stat, bf16[512,512]{1,0:T(8,128)(2,1)S(1)} %get-tuple-element.11.res_in), custom_call_target="tpu_custom_call" | custom-call | tf_op jit(solution)/shard_map/pallas_call | solution.py:327
Async XLA Ops:
  1.3 1.0 copy-start
  2.4 1.0 copy-start.1

commit v3 on v2

--- a/solution.py
+++ b/solution.py
@@ -10,6 +10,8 @@
 BLOCK = 128
 LANES = 128
 ROWS_STEP = 128
+EARLY = 0
+LAG = 2
 GRANT = 40 * 1024 * 1024
 MESH = pl.DeviceIdType.MESH
 
@@ -27,15 +29,15 @@
 
 def kernel(
     Y, Z, U, C, R, width_all,
-    att, weight, res, gain,
+    att_in, weight, res_in, gain,
     quant, stat, new_res,
     att_p, w_own, w_par, ysend, ybuf, zsend, zbuf, hid,
     l_sem, xs_sem, xr_sem, as_sem, ar_sem, ys_sem, yr_sem, zs_sem, zr_sem,
-    ss_sem, sr_sem, qzs, qzr, qys, qyr, qus, qur,
+    ss_sem, sr_sem, qzs, qzr, qys, qyr, qus, qur, att, res, al_sem, rl_sem,
 ):
     T = Y * Z
     n = T * U
-    w = res.shape[1]
+    w = res_in.shape[1]
     nb = w // BLOCK
     tp = lax.axis_index("tp")
     s = lax.axis_index("sub")
@@ -73,9 +75,13 @@
     def wpush(t):
         return rc(weight.at[:, cols(t, other)], w_par.at[t], xs_sem.at[t], xr_sem.at[t], tp, other)
 
-    apush = rc(att, att_p, as_sem, ar_sem, tp, other)
-
+    aload = pltpu.make_async_copy(att_in, att, al_sem)
+    rload = pltpu.make_async_copy(res_in, res, rl_sem)
+    apush = rc(att_in, att_p, as_sem, ar_sem, tp, other)
+
+    aload.start()
     loop(T, lambda i: wload(order(i)).start())
+    rload.start()
     barrier = pltpu.get_barrier_semaphore()
 
     def greet(k):
@@ -88,7 +94,9 @@
     pl.semaphore_wait(barrier, n - 1)
     apush.start()
     loop(T, lambda i: wpush(order(i)).start())
+    aload.wait()
     apush.wait()
+    rload.wait()
 
     def w_wait(t):
         wload(t).wait()
@@ -145,11 +153,14 @@
     def scopy(g, p, t, u, slot):
         return rc(stat.at[g, me], stat.at[g, slot], ss_sem.at[g, p], sr_sem.at[g, slot], t, u)
 
-    def qz(c, zz, right):
-        sl = quant.at[rows(c), cols(zt(zz), s)]
+    def early(c):
+        return Y > 1 and c >= C - EARLY
+
+    def qz(c, zz, right, b=0):
+        sl = quant.at[rows(c), cols(zz * Y + (yp if b else y), s)]
         to = jnp.minimum(z + 1, Z - 1) if right else jnp.maximum(z - 1, 0)
         d = 1 if right else 0
-        return rc(sl, sl, qzs.at[c, zz, d], qzr.at[c, zz], zt(to), s)
+        return rc(sl, sl, qzs.at[c, zz, d, b], qzr.at[c, zz, b], zt(to), s)
 
     def qy(c, zz, yy):
         sl = quant.at[rows(c), cols(zz * Y + yy, s)]
@@ -199,29 +210,29 @@
             loop(n - 1, send)
 
     def s7(c):
+        def hop(zz, right, b):
+            qz(c, zz, right, b).wait_recv()
+            pl.when(can_right if right else can_left)(lambda: qz(c, zz, right, b).start())
+            if Y > 1 and not early(c):
+                qy(c, zz, y).start()
+            qu(c, zz * Y + (yp if b else y), s).start()
+
+        if early(c):
+            qy(c, z, yp).wait_recv()
+            pl.when(can_right)(lambda: qz(c, z, True, 1).start())
+            pl.when(can_left)(lambda: qz(c, z, False, 1).start())
+            qu(c, z * Y + yp, s).start()
+
         def one(k):
-            lo, hi = z - (k + 1), z + (k + 1)
-
-            @pl.when(lo >= 0)
-            def _():
-                qz(c, lo, True).wait_recv()
-                pl.when(can_right)(lambda: qz(c, lo, True).start())
-                if Y > 1:
-                    qy(c, lo, y).start()
-                qu(c, zt(lo), s).start()
-
-            @pl.when(hi < Z)
-            def _():
-                qz(c, hi, False).wait_recv()
-                pl.when(can_left)(lambda: qz(c, hi, False).start())
-                if Y > 1:
-                    qy(c, hi, y).start()
-                qu(c, zt(hi), s).start()
+            for b in (0, 1) if early(c) else (0,):
+                lo, hi = z - (k + 1), z + (k + 1)
+                pl.when(lo >= 0)(lambda: hop(lo, True, b))
+                pl.when(hi < Z)(lambda: hop(hi, False, b))
 
         loop(Z - 1, one)
 
     def s8(c):
-        if Y > 1:
+        if Y > 1 and not early(c):
             def one(k):
                 zz = zo(k)
                 qy(c, zz, yp).wait_recv()
@@ -238,22 +249,26 @@
 
             loop(n - 1, w_stat)
 
-    stages = (s4, s5, s7, s8, s9)
-    for i in range(C + len(stages) - 1):
-        for j, stage in enumerate(stages):
-            if 0 <= i - j < C:
-                stage(i - j)
+    stages = ((0, s4), (1, s5), (LAG, s7), (LAG + 1, s8), (C + LAG + 1, s9))
+    for i in range(2 * C + LAG + 1):
+        for lag, stage in stages:
+            if 0 <= i - lag < C:
+                stage(i - lag)
 
     loop(T, lambda t: wpush(t).wait_send())
     for c in range(C):
         if Y > 1:
             ycopy(c).wait_send()
-            loop(Z, lambda zz, c=c: qy(c, zz, y).wait_send())
+            if early(c):
+                qy(c, z, y).wait_send()
+            else:
+                loop(Z, lambda zz, c=c: qy(c, zz, y).wait_send())
         loop(Z - 1, lambda k, c=c: zcopy(c, zo(k + 1)).wait_send())
 
         def zdone(zz, c=c):
-            pl.when(can_right & (zz <= z))(lambda: qz(c, zz, True).wait_send())
-            pl.when(can_left & (zz >= z))(lambda: qz(c, zz, False).wait_send())
+            for b in (0, 1) if early(c) else (0,):
+                pl.when(can_right & (zz <= z))(lambda: qz(c, zz, True, b).wait_send())
+                pl.when(can_left & (zz >= z))(lambda: qz(c, zz, False, b).wait_send())
 
         loop(Z, zdone)
         loop(T, lambda t, c=c: qu(c, t, s).wait_send())
@@ -294,6 +309,7 @@
     f32 = jnp.float32
     dma = pltpu.SemaphoreType.DMA
     vm = pl.BlockSpec(memory_space=pltpu.VMEM)
+    hbm = pl.BlockSpec(memory_space=pltpu.HBM)
     hb, stat, kept = pl.pallas_call(
         functools.partial(kernel, Y, Z, U, C, R, width_all),
         out_shape=(
@@ -301,7 +317,7 @@
             pltpu.VMEM((G, n, 1 + nb, LANES), f32),
             pltpu.VMEM((M, w), bf),
         ),
-        in_specs=[vm, pl.BlockSpec(memory_space=pl.ANY), vm, vm],
+        in_specs=[hbm, hbm, hbm, vm],
         out_specs=(vm, vm, vm),
         scratch_shapes=[
             pltpu.VMEM((M, K), bf),
@@ -315,7 +331,8 @@
             dma((T,)), dma((T,)), dma((T,)), dma, dma,
             dma((C,)), dma((C,)), dma((C, Z)), dma((C, Z)),
             dma((G, n)), dma((G, n)),
-            dma((C, Z, 2)), dma((C, Z)), dma((C, Z)), dma((C, Z)), dma((C, T)), dma((C, T)),
+            dma((C, Z, 2, 2)), dma((C, Z, 2)), dma((C, Z)), dma((C, Z)), dma((C, T)), dma((C, T)),
+            pltpu.VMEM((M, K), bf), pltpu.VMEM((M, w), bf), dma, dma,
         ],
         compiler_params=pltpu.CompilerParams(
             collective_id=0, has_side_effects=True, vmem_limit_bytes=GRANT

time: 132 us -> 133 us (level)
  no operation moved by 1% of the time
where the time goes in v3:
time: 133 us; the launch traced here: 132 us
  Pallas kernels  129 us (97%)
  local copies, waits for them, and re-layouts  2.77 us (2%)
    pallas_call x1, Pallas kernels, per_device(): pl.pallas_call(functools.partial(kernel, Y, Z, U, C, R, width_all), out_s...  122 us
    pallas_call x1, Pallas kernels, per_device(): pl.pallas_call(functools.partial(finish, width_all, nb), grid=(G,), out_s...  7.04 us

profile of v3, /device:TPU:1, one launch (start us, length us, event | category | flops | bytes accessed | tf_op | source)
XLA Modules:
  0.0 132.4 jit_solution(12743636799401204914)
XLA Ops:
  0.6 0.7 reshape.9.gain
  1.3 0.0 copy-start
  1.3 1.0 copy-done
  2.4 0.0 copy-start.1
  2.4 1.0 copy-done.1
  3.4 121.9 %shard_map.67 = (bf16[512,8192]{1,0:T(8,128)(2,1)S(1)}, f32[4,16,5,128]{3,2,1,0:T(8,128)S(1)}, bf16[512,512]{1,0:T(8,128)(2,1)S(1)}) custom-call(bf16[512,512]{1,0:T(8,128)(2,1)S(1)} %copy-done, bf16[512,8192]{1,0:T(8,128)(2,1)} %weight.1, bf16[512,512]{1,0:T(8,128)(2,1)S(1)} %copy-done.1, bf16[1,512]{1,0:T(2,128)(2,1)S(1)} %reshape.9.gain), custom_call_target="tpu_custom_call" | custom-call | flops 4294967296 | bytes 8388608 | tf_op jit(solution)/shard_map/pallas_call | solution.py:313
  125.3 7.0 %shard_map.68 = (bf16[512,8192]{1,0:T(8,128)(2,1)}, bf16[64,512]{1,0:T(8,128)(2,1)}, bf16[512,512]{1,0:T(8,128)(2,1)}) custom-call(bf16[512,8192]{1,0:T(8,128)(2,1)S(1)} %get-tuple-element.9.hb, f32[4,16,5,128]{3,2,1,0:T(8,128)S(1)} %get-tuple-element.10.stat, bf16[512,512]{1,0:T(8,128)(2,1)S(1)} %get-tuple-element.11.res_in), custom_call_target="tpu_custom_call" | custom-call | tf_op jit(solution)/shard_map/pallas_call | solution.py:344
Async XLA Ops:
  1.3 1.0 copy-start
  2.4 1.0 copy-start.1
